TPU v7x, 16 devices: a 4x2x1 block of a 4x4x8 slice. The times are simulated.
16 devices in a mesh: batch: 2 (over y, z), time: 8 (over x, core).
Axes of the slice: x: 4, y: 2, z: 1, core: 2. Of those that a mesh axis runs over, the one named last changes fastest.
The devices are a block of a 4x4x8 slice.
Arguments:
- latent: bfloat16 [768, 4, 48, 128], P(('batch', 'time')), parts along dimension 0
- conv_w: bfloat16 [4, 3, 3, 3, 128, 128], replicated
- conv_b: float32 [4, 128], replicated
- norm_g: float32 [5, 128], replicated
- norm_b: float32 [5, 128], replicated
- attn_w: bfloat16 [4, 128, 128], replicated
- attn_b: float32 [4, 128], replicated
Outputs:
- output: bfloat16 [768, 4, 48, 128], P(('batch', 'time')), parts along dimension 0
There are 2 independent parts. A program takes and returns all parts, laid end to end along the dimension named above; an argument that names none is the same for every part.
All inputs are finite; a program needn't handle non-finite values.
Results may differ from a plain program's by a relative error of at most 0.0139455.
Values are sent between devices in bfloat16 or wider.
A program may use at most 768 MiB of HBM per device.

v0:
```python
import functools

import jax
import jax.numpy as jnp
from jax import lax
from jax.experimental import pallas as pl
from jax.experimental.pallas import tpu as pltpu
from jax.sharding import PartitionSpec as P

GROUPS = 32
NORM_EPS = 1e-6
TILE = 8
ATT = 2
CHUNKS = 4
HALO = 2
MESH_ID = pl.DeviceIdType.MESH
F32, BF16 = jnp.float32, jnp.bfloat16


def dot(a, b):
    return jnp.dot(a, b, preferred_element_type=F32)


def vreg_sum(value):
    return jnp.sum(value.reshape(-1, 8, value.shape[-1]), axis=0)


def kernel(n_dev, latent, conv_w, conv_b, norm_g, norm_b, attn_w, attn_b, out, x_ref, h_ref, ua, ub, w_ref, aw_ref, cb_ref, g_ref, b_ref, ab_ref, halo, stats, in_sem, par_sem, out_sem, halo_send, halo_recv, stat_send, stat_recv):
    frames, height, width, chan = latent.shape
    me = lax.axis_index("time")
    tiles = frames // TILE
    piece = frames // CHUNKS
    elem_count = n_dev * frames * height * width * (chan // GROUPS)

    in_copies = [pltpu.make_async_copy(latent.at[pl.ds(c * piece, piece)], x_ref.at[pl.ds(HALO + c * piece, piece)], in_sem.at[c]) for c in range(CHUNKS)]
    for c in reversed(range(CHUNKS)):
        in_copies[c].start()
    pairs = [(norm_g, g_ref), (norm_b, b_ref), (conv_b, cb_ref), (attn_w, aw_ref), (attn_b, ab_ref), (conv_w, w_ref)]
    par_copies = [pltpu.make_async_copy(src, dst, par_sem.at[i]) for i, (src, dst) in enumerate(pairs)]
    for copy in par_copies:
        copy.start()

    barrier = pltpu.get_barrier_semaphore()
    for k in range(1, n_dev):
        pl.semaphore_signal(barrier, inc=1, device_id={"time": lax.rem(me + k, n_dev)}, device_id_type=MESH_ID)
    pl.semaphore_wait(barrier, n_dev - 1)

    def halo_copy(slot, src, start):
        return pltpu.make_async_remote_copy(src_ref=src.at[pl.ds(start, HALO)], dst_ref=halo.at[slot], send_sem=halo_send.at[slot], recv_sem=halo_recv.at[slot], device_id={"time": lax.rem(me + 1, n_dev)}, device_id_type=MESH_ID)

    def send_halo(slot, src):
        @pl.when(me < n_dev - 1)
        def _():
            halo_copy(slot, src, frames).start()

    def take_halo(slot, src):
        @pl.when(me > 0)
        def _():
            halo_copy(slot, src, frames).wait_recv()
            src[pl.ds(0, HALO)] = halo[slot]

        @pl.when(me == 0)
        def _():
            for f in range(HALO):
                src[f] = src[HALO]

        @pl.when(me < n_dev - 1)
        def _():
            halo_copy(slot, src, frames).wait_send()

    lane = lax.broadcasted_iota(jnp.int32, (8, chan), 1)

    def exchange(stage, sums):
        both = jnp.concatenate([jnp.sum(sums[0], axis=0, keepdims=True), jnp.sum(sums[1], axis=0, keepdims=True), jnp.zeros((6, chan), F32)], axis=0)
        stats[stage, me] = both

        def copy_to(k):
            return pltpu.make_async_remote_copy(src_ref=stats.at[stage, me], dst_ref=stats.at[stage, me], send_sem=stat_send.at[stage, k], recv_sem=stat_recv.at[stage, n_dev - k], device_id={"time": lax.rem(me + k, n_dev)}, device_id_type=MESH_ID)

        def copy_from(k):
            peer = lax.rem(me + k, n_dev)
            return pltpu.make_async_remote_copy(src_ref=stats.at[stage, peer], dst_ref=stats.at[stage, peer], send_sem=stat_send.at[stage, k], recv_sem=stat_recv.at[stage, k], device_id={"time": peer}, device_id_type=MESH_ID)

        for k in range(1, n_dev):
            copy_to(k).start()
        for k in range(1, n_dev):
            copy_from(k).wait_recv()
        total = stats[stage, 0]
        for d in range(1, n_dev):
            total = total + stats[stage, d]
        for k in range(1, n_dev):
            copy_to(k).wait_send()
        per_group = chan // GROUPS
        step = 1
        while step < per_group:
            swap = jnp.where(lax.rem(lane, 2 * step) < step, pltpu.roll(total, chan - step, 1), pltpu.roll(total, step, 1))
            total = total + swap
            step *= 2
        mean = total[0:1] / elem_count
        inv_std = lax.rsqrt(total[1:2] / elem_count - mean * mean + NORM_EPS)
        return mean, inv_std * g_ref[pl.ds(stage, 1)], b_ref[pl.ds(stage, 1)]

    col = lax.rem(lax.broadcasted_iota(jnp.int32, (height * width, chan), 0), width)

    def norm_tile(src, dst, tile, coef):
        mean, scale, shift = coef
        for f in range(TILE + HALO):
            value = src[tile * TILE + f].astype(F32).reshape(height * width, chan)
            half = 0.5 * ((value - mean) * scale + shift)
            act = half + half * jnp.tanh(half)
            left = jnp.where(col == 0, 0.0, pltpu.roll(act, 1, 0))
            right = jnp.where(col == width - 1, 0.0, pltpu.roll(act, height * width - 1, 0))
            for e, moved in enumerate((left, act, right)):
                dst[:, f, :, e * chan:(e + 1) * chan] = moved.astype(BF16).reshape(height, width, chan)

    zero_w = jnp.zeros((chan, chan), BF16)

    def conv_tile(u, k, bias):
        def cols(row, first, count, e):
            return u[row, first:first + count, :, e * chan:(e + 1) * chan].reshape(count * width, chan)

        lhs, rhs = [], []
        for a in range(3):
            for e in range(3):
                for side in range(2):
                    lhs.append(jnp.concatenate([cols(g + side, a, TILE, e) for g in range(0, height, 2)], axis=0))
                    rhs.append(jnp.concatenate([w_ref[k, a, 1 + side, e], w_ref[k, a, side, e]], axis=1))
        main = dot(jnp.concatenate(lhs, axis=1), jnp.concatenate(rhs, axis=0))

        def extra(row, d):
            lhs, rhs = [], []
            for s in range(4):
                for e in range(3):
                    lhs.append(jnp.concatenate([cols(row, 2 * p + s, 1, e) for p in range(TILE // 2)], axis=0))
                    rhs.append(jnp.concatenate([w_ref[k, s, d, e] if s < 3 else zero_w, w_ref[k, s - 1, d, e] if s > 0 else zero_w], axis=1))
            return dot(jnp.concatenate(lhs, axis=1), jnp.concatenate(rhs, axis=0))

        lower = extra(2, 2)
        upper = extra(1, 0)
        rows = []
        for f in range(TILE):
            here = slice(f * width, (f + 1) * width)
            there = slice((TILE + f) * width, (TILE + f + 1) * width)
            pair = slice((f // 2) * width, (f // 2 + 1) * width)
            half = slice((f % 2) * chan, (f % 2 + 1) * chan)
            rows.append([main[here, :chan] + bias, main[here, chan:] + lower[pair, half] + bias, main[there, :chan] + upper[pair, half] + bias, main[there, chan:] + bias])
        return rows

    def conv_stage(k, src, coef, emit, after):
        bias = cb_ref[pl.ds(k, 1)]
        norm_tile(src, ua, tiles - 1, coef)

        def finish(u, tile, sums):
            rows = conv_tile(u, k, bias)
            for f in range(TILE):
                for i in range(height):
                    value = emit(tile * TILE + f, i, rows[f][i].astype(BF16)).astype(F32)
                    sums = (sums[0] + vreg_sum(value), sums[1] + vreg_sum(value * value))
            return sums

        def body(it, sums):
            high = tiles - 1 - 2 * it
            norm_tile(src, ub, high - 1, coef)
            sums = finish(ua, high, sums)
            norm_tile(src, ua, jnp.maximum(high - 2, 0), coef)
            sums = finish(ub, high - 1, sums)
            after(it, high)
            return sums

        zero = jnp.zeros((8, chan), F32)
        return lax.fori_loop(0, tiles // 2, body, (zero, zero))

    def into_h(frame, i, value):
        h_ref[HALO + frame, i] = value
        return value

    def into_x(frame, i, value):
        value = (x_ref[HALO + frame, i].astype(F32) + value.astype(F32)).astype(BF16)
        x_ref[HALO + frame, i] = value
        return value

    def send_first(slot, src):
        def after(it, high):
            @pl.when(it == 0)
            def _():
                send_halo(slot, src)
        return after

    def nothing(it, high):
        pass

    def out_copy(it):
        first = frames - 2 * TILE * (it + 1)
        return pltpu.make_async_copy(x_ref.at[pl.ds(HALO + first, 2 * TILE)], out.at[pl.ds(first, 2 * TILE)], out_sem.at[it])

    def write_out(it, high):
        out_copy(it).start()

    zero = jnp.zeros((8, chan), F32)
    sums = (zero, zero)
    for c in reversed(range(CHUNKS)):
        in_copies[c].wait()
        if c == CHUNKS - 1:
            send_halo(0, x_ref)

        def add_frame(f, sums):
            value = x_ref[HALO + c * piece + f].astype(F32)
            return sums[0] + vreg_sum(value), sums[1] + vreg_sum(value * value)

        sums = lax.fori_loop(0, piece, add_frame, sums)
    for copy in par_copies:
        copy.wait()

    coef = exchange(0, sums)
    take_halo(0, x_ref)
    sums = conv_stage(0, x_ref, coef, into_h, send_first(1, h_ref))
    coef = exchange(1, sums)
    take_halo(1, h_ref)
    sums = conv_stage(1, h_ref, coef, into_x, nothing)
    mean, scale, shift = exchange(2, sums)

    tokens = height * width
    qkv_w = jnp.concatenate([aw_ref[0], aw_ref[1], aw_ref[2]], axis=1)
    qkv_b = jnp.concatenate([ab_ref[0:1], ab_ref[1:2], ab_ref[2:3]], axis=1)
    out_b = ab_ref[3:4]
    gain = chan ** -0.5 * 1.4426950408889634

    def attend(it, sums):
        first = frames - ATT * (it + 1)
        feature = x_ref[pl.ds(HALO + first, ATT)].astype(F32).reshape(ATT * tokens, chan)
        normed = ((feature - mean) * scale + shift).astype(BF16)
        qkv = (dot(normed, qkv_w) + qkv_b).astype(BF16)
        mixed = []
        for f in range(ATT):
            mine = slice(f * tokens, (f + 1) * tokens)
            scores = lax.dot_general(qkv[mine, :chan], qkv[mine, chan:2 * chan], (((1,), (1,)), ((), ())), preferred_element_type=F32)
            power = jnp.exp2((scores - jnp.max(scores, axis=1, keepdims=True)) * gain)
            probs = (power / jnp.sum(power, axis=1, keepdims=True)).astype(BF16)
            mixed.append(dot(probs, qkv[mine, 2 * chan:]).astype(BF16))
        branch = (dot(jnp.concatenate(mixed, axis=0), aw_ref[3]) + out_b).astype(BF16)
        value = (feature + branch.astype(F32)).astype(BF16)
        x_ref[pl.ds(HALO + first, ATT)] = value.reshape(ATT, height, width, chan)

        @pl.when(it == max(1, HALO // ATT))
        def _():
            send_halo(2, x_ref)

        value = value.astype(F32)
        return sums[0] + vreg_sum(value), sums[1] + vreg_sum(value * value)

    sums = lax.fori_loop(0, frames // ATT, attend, (zero, zero))
    coef = exchange(3, sums)
    take_halo(2, x_ref)
    sums = conv_stage(2, x_ref, coef, into_h, send_first(3, h_ref))
    coef = exchange(4, sums)
    take_halo(3, h_ref)
    conv_stage(3, h_ref, coef, into_x, write_out)
    for it in range(tiles // 2):
        out_copy(it).wait()


def solution(mesh):
    n_dev = mesh.shape["time"]
    video_spec = P(("batch", "time"), None, None, None)

    def device_body(latent, conv_w, conv_b, norm_g, norm_b, attn_w, attn_b):
        frames, height, width, chan = latent.shape
        anywhere = pl.BlockSpec(memory_space=pl.ANY)
        padded = (frames + HALO, height, width, chan)
        tile_shape = (height, TILE + HALO, width, 3 * chan)
        dma = pltpu.SemaphoreType.DMA
        return pl.pallas_call(
            functools.partial(kernel, n_dev),
            out_shape=jax.ShapeDtypeStruct(latent.shape, latent.dtype),
            in_specs=[anywhere] * 7,
            out_specs=anywhere,
            scratch_shapes=[
                pltpu.VMEM(padded, BF16),
                pltpu.VMEM(padded, BF16),
                pltpu.VMEM(tile_shape, BF16),
                pltpu.VMEM(tile_shape, BF16),
                pltpu.VMEM(conv_w.shape, BF16),
                pltpu.VMEM(attn_w.shape, BF16),
                pltpu.VMEM(conv_b.shape, F32),
                pltpu.VMEM(norm_g.shape, F32),
                pltpu.VMEM(norm_b.shape, F32),
                pltpu.VMEM(attn_b.shape, F32),
                pltpu.VMEM((4, HALO, height, width, chan), BF16),
                pltpu.VMEM((5, n_dev, 8, chan), F32),
                dma((CHUNKS,)),
                dma((6,)),
                dma((frames // TILE // 2,)),
                dma((4,)),
                dma((4,)),
                dma((5, n_dev)),
                dma((5, n_dev)),
            ],
            compiler_params=pltpu.CompilerParams(collective_id=0, has_side_effects=True),
        )(latent, conv_w, conv_b, norm_g, norm_b, attn_w, attn_b)

    return jax.shard_map(device_body, mesh=mesh, in_specs=(video_spec, P(), P(), P(), P(), P(), P()), out_specs=video_spec, check_vma=False)
```

profile of v0, /device:TPU:113, one launch (start us, length us, event | category | flops | bytes accessed | tf_op | source)
XLA Modules:
  0.0 90.6 jit_solution(802831692801738904)
XLA Ops:
  0.0 87.1 %shard_map.73 = bf16[48,4,48,128]{3,2,1,0:T(8,128)(2,1)} custom-call(bf16[48,4,48,128]{3,2,1,0:T(8,128)(2,1)} %latent.1, bf16[4,3,3,3,128,128]{5,4,3,2,1,0:T(8,128)(2,1)} %conv_w.1, f32[4,128]{1,0:T(4,128)} %conv_b.1, f32[5,128]{1,0:T(8,128)} %norm_g.1, f32[5,128]{1,0:T(8,128)} %norm_b.1, bf16[4,128,128]{2,1,0:T(8,128)(2,1)} %attn_w.1, f32[4,128]{1,0:T(4,128)} %attn_b.1), custom_call_target="tpu_custom_call" | custom-call | tf_op jit(solution)/shard_map/pallas_call | solution.py:272
  87.1 3.5 %copy.9 = bf16[48,4,48,128]{3,2,1,0:T(8,128)(2,1)} copy(bf16[48,4,48,128]{3,2,1,0:T(8,128)(2,1)} %shard_map.73) | data formatting | bytes 4718592
where the time goes:
time: 90.7 us; the launch traced here: 90.6 us
  Pallas kernels  87.1 us (96%)
  local copies, waits for them, and re-layouts  3.48 us (4%)
    pallas_call x1, Pallas kernels, device_body(): pl.pallas_call(functools.partial(kernel, n_dev), out_shape=jax.ShapeDtype...  87.1 us
    unnamed x1, local copies, waits for them, and re-layouts  3.48 us

commit v1 on v0

--- a/solution.py
+++ b/solution.py
@@ -10,7 +10,7 @@
 GROUPS = 32
 NORM_EPS = 1e-6
 TILE = 8
-ATT = 2
+ATT = 8
 CHUNKS = 4
 HALO = 2
 MESH_ID = pl.DeviceIdType.MESH
@@ -25,7 +25,7 @@
     return jnp.sum(value.reshape(-1, 8, value.shape[-1]), axis=0)
 
 
-def kernel(n_dev, latent, conv_w, conv_b, norm_g, norm_b, attn_w, attn_b, out, x_ref, h_ref, ua, ub, w_ref, aw_ref, cb_ref, g_ref, b_ref, ab_ref, halo, stats, in_sem, par_sem, out_sem, halo_send, halo_recv, stat_send, stat_recv):
+def kernel(n_dev, latent, conv_w, conv_b, norm_g, norm_b, attn_w, attn_b, out, x_ref, h_ref, ua, ub, act_a, act_b, w_ref, aw_ref, cb_ref, g_ref, b_ref, ab_ref, halo, stats, in_sem, par_sem, out_sem, halo_send, halo_recv, stat_send, stat_recv):
     frames, height, width, chan = latent.shape
     me = lax.axis_index("time")
     tiles = frames // TILE
@@ -43,7 +43,8 @@
     barrier = pltpu.get_barrier_semaphore()
     for k in range(1, n_dev):
         pl.semaphore_signal(barrier, inc=1, device_id={"time": lax.rem(me + k, n_dev)}, device_id_type=MESH_ID)
-    pl.semaphore_wait(barrier, n_dev - 1)
+    with jax.named_scope('barrier'):
+        pl.semaphore_wait(barrier, n_dev - 1)
 
     def halo_copy(slot, src, start):
         return pltpu.make_async_remote_copy(src_ref=src.at[pl.ds(start, HALO)], dst_ref=halo.at[slot], send_sem=halo_send.at[slot], recv_sem=halo_recv.at[slot], device_id={"time": lax.rem(me + 1, n_dev)}, device_id_type=MESH_ID)
@@ -100,18 +101,26 @@
         inv_std = lax.rsqrt(total[1:2] / elem_count - mean * mean + NORM_EPS)
         return mean, inv_std * g_ref[pl.ds(stage, 1)], b_ref[pl.ds(stage, 1)]
 
-    col = lax.rem(lax.broadcasted_iota(jnp.int32, (height * width, chan), 0), width)
-
-    def norm_tile(src, dst, tile, coef):
+    block = width + 8
+    for act in (act_a, act_b):
+        for f in range(TILE + HALO):
+            for i in range(height + 1):
+                act[f, i * block:i * block + 8] = jnp.zeros((8, chan), F32)
+
+    def norm_tile(src, dst, act, tile, coef):
         mean, scale, shift = coef
+        scale, shift = 0.5 * scale, 0.5 * shift
         for f in range(TILE + HALO):
-            value = src[tile * TILE + f].astype(F32).reshape(height * width, chan)
-            half = 0.5 * ((value - mean) * scale + shift)
-            act = half + half * jnp.tanh(half)
-            left = jnp.where(col == 0, 0.0, pltpu.roll(act, 1, 0))
-            right = jnp.where(col == width - 1, 0.0, pltpu.roll(act, height * width - 1, 0))
-            for e, moved in enumerate((left, act, right)):
-                dst[:, f, :, e * chan:(e + 1) * chan] = moved.astype(BF16).reshape(height, width, chan)
+            value = src[tile * TILE + f].astype(F32)
+            half = (value - mean) * scale + shift
+            value = half + half * jnp.tanh(half)
+            dst[:, f, :, chan:2 * chan] = value.astype(BF16)
+            for i in range(height):
+                act[f, i * block + 8:(i + 1) * block] = value[i]
+            for i in range(height):
+                for e in (0, 2):
+                    moved = act[f, i * block + 7 + e:i * block + 7 + e + width]
+                    dst[i, f, :, e * chan:(e + 1) * chan] = moved.astype(BF16)
 
     zero_w = jnp.zeros((chan, chan), BF16)
 
@@ -148,7 +157,8 @@
 
     def conv_stage(k, src, coef, emit, after):
         bias = cb_ref[pl.ds(k, 1)]
-        norm_tile(src, ua, tiles - 1, coef)
+        with jax.named_scope('norm_first'):
+            norm_tile(src, ua, act_a, tiles - 1, coef)
 
         def finish(u, tile, sums):
             rows = conv_tile(u, k, bias)
@@ -160,9 +170,9 @@
 
         def body(it, sums):
             high = tiles - 1 - 2 * it
-            norm_tile(src, ub, high - 1, coef)
+            norm_tile(src, ub, act_b, high - 1, coef)
             sums = finish(ua, high, sums)
-            norm_tile(src, ua, jnp.maximum(high - 2, 0), coef)
+            norm_tile(src, ua, act_a, jnp.maximum(high - 2, 0), coef)
             sums = finish(ub, high - 1, sums)
             after(it, high)
             return sums
@@ -208,16 +218,24 @@
             return sums[0] + vreg_sum(value), sums[1] + vreg_sum(value * value)
 
         sums = lax.fori_loop(0, piece, add_frame, sums)
-    for copy in par_copies:
-        copy.wait()
-
-    coef = exchange(0, sums)
-    take_halo(0, x_ref)
-    sums = conv_stage(0, x_ref, coef, into_h, send_first(1, h_ref))
-    coef = exchange(1, sums)
-    take_halo(1, h_ref)
-    sums = conv_stage(1, h_ref, coef, into_x, nothing)
-    mean, scale, shift = exchange(2, sums)
+    with jax.named_scope('par_wait'):
+        for copy in par_copies:
+            copy.wait()
+
+    with jax.named_scope('exchange0'):
+        coef = exchange(0, sums)
+    with jax.named_scope('halo0'):
+        take_halo(0, x_ref)
+    with jax.named_scope('conv0'):
+        sums = conv_stage(0, x_ref, coef, into_h, send_first(1, h_ref))
+    with jax.named_scope('exchange1'):
+        coef = exchange(1, sums)
+    with jax.named_scope('halo1'):
+        take_halo(1, h_ref)
+    with jax.named_scope('conv1'):
+        sums = conv_stage(1, h_ref, coef, into_x, nothing)
+    with jax.named_scope('exchange2'):
+        mean, scale, shift = exchange(2, sums)
 
     tokens = height * width
     qkv_w = jnp.concatenate([aw_ref[0], aw_ref[1], aw_ref[2]], axis=1)
@@ -248,15 +266,23 @@
         value = value.astype(F32)
         return sums[0] + vreg_sum(value), sums[1] + vreg_sum(value * value)
 
-    sums = lax.fori_loop(0, frames // ATT, attend, (zero, zero))
-    coef = exchange(3, sums)
-    take_halo(2, x_ref)
-    sums = conv_stage(2, x_ref, coef, into_h, send_first(3, h_ref))
-    coef = exchange(4, sums)
-    take_halo(3, h_ref)
-    conv_stage(3, h_ref, coef, into_x, write_out)
-    for it in range(tiles // 2):
-        out_copy(it).wait()
+    with jax.named_scope('attention'):
+        sums = lax.fori_loop(0, frames // ATT, attend, (zero, zero))
+    with jax.named_scope('exchange3'):
+        coef = exchange(3, sums)
+    with jax.named_scope('halo2'):
+        take_halo(2, x_ref)
+    with jax.named_scope('conv2'):
+        sums = conv_stage(2, x_ref, coef, into_h, send_first(3, h_ref))
+    with jax.named_scope('exchange4'):
+        coef = exchange(4, sums)
+    with jax.named_scope('halo3'):
+        take_halo(3, h_ref)
+    with jax.named_scope('conv3'):
+        conv_stage(3, h_ref, coef, into_x, write_out)
+    with jax.named_scope('drain'):
+        for it in range(tiles // 2):
+            out_copy(it).wait()
 
 
 def solution(mesh):
@@ -268,6 +294,7 @@
         anywhere = pl.BlockSpec(memory_space=pl.ANY)
         padded = (frames + HALO, height, width, chan)
         tile_shape = (height, TILE + HALO, width, 3 * chan)
+        act_shape = (TILE + HALO, height * (width + 8) + 8, chan)
         dma = pltpu.SemaphoreType.DMA
         return pl.pallas_call(
             functools.partial(kernel, n_dev),
@@ -279,6 +306,8 @@
                 pltpu.VMEM(padded, BF16),
                 pltpu.VMEM(tile_shape, BF16),
                 pltpu.VMEM(tile_shape, BF16),
+                pltpu.VMEM(act_shape, F32),
+                pltpu.VMEM(act_shape, F32),
                 pltpu.VMEM(conv_w.shape, BF16),
                 pltpu.VMEM(attn_w.shape, BF16),
                 pltpu.VMEM(conv_b.shape, F32),

time: 90.7 us -> 77.7 us (0.86)
  Pallas kernels: 87.1 us -> 74.1 us
    pallas_call x1, Pallas kernels: 87.1 us -> 74.1 us  [device_body(): pl.pallas_call(functools.partial(kernel, n_dev), out_shape=jax.ShapeDtype...]
where the time goes in v1:
time: 77.7 us; the launch traced here: 77.6 us
  Pallas kernels  74.1 us (95%)
  local copies, waits for them, and re-layouts  3.48 us (4%)
    pallas_call x1, Pallas kernels, device_body(): pl.pallas_call(functools.partial(kernel, n_dev), out_shape=jax.ShapeDtype...  74.1 us
    unnamed x1, local copies, waits for them, and re-layouts  3.48 us

profile of v1, /device:TPU:113, one launch (start us, length us, event | category | flops | bytes accessed | tf_op | source)
XLA Modules:
  0.0 77.6 jit_solution(1595647208086012789)
XLA Ops:
  0.0 74.1 %shard_map.73 = bf16[48,4,48,128]{3,2,1,0:T(8,128)(2,1)} custom-call(bf16[48,4,48,128]{3,2,1,0:T(8,128)(2,1)} %latent.1, bf16[4,3,3,3,128,128]{5,4,3,2,1,0:T(8,128)(2,1)} %conv_w.1, f32[4,128]{1,0:T(4,128)} %conv_b.1, f32[5,128]{1,0:T(8,128)} %norm_g.1, f32[5,128]{1,0:T(8,128)} %norm_b.1, bf16[4,128,128]{2,1,0:T(8,128)(2,1)} %attn_w.1, f32[4,128]{1,0:T(4,128)} %attn_b.1), custom_call_target="tpu_custom_call" | custom-call | tf_op jit(solution)/shard_map/pallas_call | solution.py:299
  74.1 3.5 %copy.9 = bf16[48,4,48,128]{3,2,1,0:T(8,128)(2,1)} copy(bf16[48,4,48,128]{3,2,1,0:T(8,128)(2,1)} %shard_map.73) | data formatting | bytes 4718592
